TPU v7x, 512 devices: a whole 4x8x8 slice. The times are simulated.
512 devices in a mesh: dp: 32 (over x, y), tensor: 16 (over z, core).
Axes of the slice: x: 4, y: 8, z: 8, core: 2. Of those that a mesh axis runs over, the one named last changes fastest.
Arguments:
- acts: bfloat16 [32768, 256], P('dp'), may hold values from -6 to 6
- out_grad: bfloat16 [32768, 16384], P('dp', 'tensor'), may hold values from -6 to 6
- weight: float32 [256, 16384], P(None, 'tensor'), may hold values from -0.375 to 0.375
- error: float32 [32, 256, 16384], P('dp', None, 'tensor'), may hold values from -6 to 6
- start_q: float32 [16384, 64], P('tensor'), may hold values from -0.1875 to 0.1875
Outputs:
- new_weight: float32 [256, 16384], P(None, 'tensor')
- new_error: float32 [32, 256, 16384], P('dp', None, 'tensor')
- input_grad: float32 [32768, 256], P(('dp', 'tensor'))
All inputs are finite; a program needn't handle non-finite values.
Results may differ from a plain program's by a relative error of at most 0.0003.
Values sent between devices are 32-bit elements; how exact they have to be, the bound alone decides.
A program may use at most 64 MiB of HBM per device.

v0:
```python
import math

import jax
import jax.numpy as jnp
from jax import lax
from jax.sharding import PartitionSpec as P

HIGH = lax.Precision.HIGHEST


def in_blocks(shard, dim, devices):
    lengths = shard.shape
    parts = shard.reshape(*lengths[:dim], devices, lengths[dim] // devices, *lengths[dim + 1 :])
    return jnp.moveaxis(parts, dim, 0)


def sum_at_owner(shard, axis, dim):
    parts = in_blocks(shard, dim, lax.axis_size(axis))
    arrived = lax.all_to_all(parts, axis, split_axis=0, concat_axis=0, tiled=True)
    return arrived.sum(axis=0)


def padded_to(lines, devices):
    spare = -lines.shape[0] % devices
    if not spare:
        return lines
    return jnp.concatenate([lines, jnp.zeros((spare, *lines.shape[1:]), lines.dtype)])


def copy_for_each(shard, axis):
    devices = lax.axis_size(axis)
    return lax.all_to_all(
        jnp.broadcast_to(shard[None], (devices, *shard.shape)), axis, 0, 0, tiled=True
    )


def in_order(parts, dim):
    parts = jnp.moveaxis(parts, 0, dim)
    lengths = parts.shape
    return parts.reshape(*lengths[:dim], lengths[dim] * lengths[dim + 1], *lengths[dim + 2 :])


def collect(shard, axis, dim):
    parts = copy_for_each(shard, axis)
    return in_order(parts, dim)


def nested_sum(shard, axes):
    lines = shard.reshape(-1, shard.shape[-1])
    own = sum_at_owner(padded_to(lines, lax.axis_size(axes)), axes, 0)
    whole = collect(own, axes, 0)
    return whole[: len(lines)].reshape(shard.shape)


def local(acts, out_grad, weight, error, start_q):
    tok_rows = acts.shape[0]
    replicas = lax.axis_size("dp")
    gradient = jnp.einsum(
        "td,tc->dc", acts, out_grad, preferred_element_type=jnp.float32
    ) / math.sqrt(tok_rows)
    merged = gradient + error[0]
    left = nested_sum(jnp.dot(merged, start_q, precision=HIGH), "dp") / replicas
    gram = jnp.dot(left.T, left, precision=HIGH)
    chol = jnp.linalg.cholesky(gram)
    ortho = jax.scipy.linalg.solve_triangular(chol, left.T, lower=True).T
    right = nested_sum(jnp.dot(merged.T, ortho, precision=HIGH), "dp") / replicas
    delta = jnp.dot(ortho, right.T, precision=HIGH)
    new_error = (merged - delta)[None]
    new_weight = weight - delta
    partial_sum = jnp.dot(out_grad.astype(jnp.float32), weight.T, precision=HIGH)
    input_grad = sum_at_owner(partial_sum, "tensor", 0)
    return (new_weight, new_error, input_grad)


def solution(mesh):
    placed = (
        P("dp", None),
        P("dp", "tensor"),
        P(None, "tensor"),
        P("dp", None, "tensor"),
        P("tensor", None),
    )
    return jax.shard_map(
        local,
        mesh=mesh,
        in_specs=placed,
        out_specs=(P(None, "tensor"), P("dp", None, "tensor"), P(("dp", "tensor"), None)),
        check_vma=False,
    )
```

profile of v0, /device:TPU:1, one launch (start us, length us, event | category | flops | bytes accessed | tf_op | source)
XLA Modules:
  0.0 137.6 jit_solution(684486160322263070)
XLA Ops:
  0.7 1.6 %copy-done = bf16[1024,1024]{1,0:T(8,128)(2,1)S(1)} copy-done((bf16[1024,1024]{1,0:T(8,128)(2,1)S(1)}, bf16[1024,1024]{1,0:T(8,128)(2,1)}, u32[]{:S(2)}) %copy-start) | copy-done | bytes 2097176
  2.2 2.1 %fusion = f32[256,1024]{1,0:T(8,128)S(1)} fusion(bf16[1024,256]{1,0:T(8,128)(2,1)} %param.5, bf16[1024,1024]{1,0:T(8,128)(2,1)S(1)} %copy-done, f32[1,256,1024]{2,1,0:T(8,128)} %param.8), kind=kOutput, calls=%fused_computation.1 | convolution fusion | flops 537395200 | bytes 4718592 | tf_op jit(solution)/shard_map/td,tc->dc/dot_general | solution.py:58
  4.4 1.0 convolution_bitcast_fusion
  5.5 19.1 %all_to_all.25 = f32[32,1,512]{2,1,0:T(1,128)S(1)} all-to-all(f32[32,1,512]{2,1,0:T(1,128)S(1)} %reshape.38), channel_id=1, replica_groups=mesh['dp'=32,'tensor'=16] {'dp'}, dimensions={0} | all-to-all | bytes 131072 | tf_op jit(solution)/shard_map/all_to_all | solution.py:19
  24.6 0.5 broadcast.63
  25.1 0.8 reduce.6
  26.2 12.0 %all_to_all.26 = f32[32,1,512]{2,1,0:T(1,128)S(1)} all-to-all(f32[32,1,512]{2,1,0:T(1,128)S(1)} %reshape.40), channel_id=1, replica_groups=mesh['dp'=32,'tensor'=16] {'dp'}, dimensions={0} | all-to-all | bytes 131072 | tf_op jit(solution)/shard_map/all_to_all | solution.py:32
  38.2 0.8 reduce.7
  39.1 0.4 convolution_bitcast_fusion.1
  39.6 5.8 %cholesky.16 = f32[64,64]{1,0:T(8,128)S(1)} custom-call(f32[64,64]{1,0:T(8,128)S(1)} %fusion.6), custom_call_target="Cholesky" | custom-call | tf_op jit(solution)/shard_map/jit(cholesky)/cholesky | solution.py:64
  45.5 0.6 compare_reduce_fusion
  46.2 0.7 fusion.4
  46.8 4.9 %custom-call.7 = f32[1,64,64]{1,2,0:T(8,128)S(1)} custom-call(f32[1,64,64]{2,1,0:T(8,128)S(1)} %fusion.4), custom_call_target="InvertDiagBlocksLowerTriangular" | custom-call | tf_op jit(solution)/shard_map/jit(_solve_triangular)/triangular_solve | solution.py:65
  52.1 2.6 %fusion.7 = f32[1024,64]{1,0:T(8,128)} fusion(f32[256,1024]{1,0:T(8,128)S(1)} %fusion, f32[64,256]{1,0:T(8,128)S(1)} %fusion.1), kind=kOutput, calls=%fused_computation.19 | convolution fusion | flops 201326592 | bytes 1376256 | tf_op jit(solution)/shard_map/dot_general | solution.py:66
  54.7 1.4 reshape.42
  56.0 13.5 %all_to_all.27 = f32[32,1,2048]{2,1,0:T(1,128)} all-to-all(f32[32,1,2048]{2,1,0:T(1,128)S(1)} %reshape.42), channel_id=1, replica_groups=mesh['dp'=32,'tensor'=16] {'dp'}, dimensions={0} | all-to-all | bytes 524288 | tf_op jit(solution)/shard_map/all_to_all | solution.py:19
  69.5 2.2 %reduce.8 = f32[32,2048]{1,0:T(8,128)S(1)} reduce(f32[32,1,2048]{2,1,0:T(1,128)} %all_to_all.27, f32[]{:T(128)} %broadcast.63), dimensions={1}, to_apply=%all_to_all.17.reduce_sub_computation | reduce | bytes 524292 | tf_op jit(solution)/shard_map/all_to_all | solution.py:19
  71.7 1.0 reshape.43
  72.8 1.1 reduce_sum.28
  73.8 0.9 broadcast_in_dim.9
  74.7 2.1 %reshape.44 = f32[32,1,2048]{2,1,0:T(1,128)} reshape(f32[32,32,64]{2,1,0:T(8,128)} %broadcast_in_dim.9) | data formatting | bytes 524288
  76.8 4.4 %all-to-all-start.3 = ((f32[32,1,2048]{2,1,0:T(1,128)}), f32[32,1,2048]{2,1,0:T(1,128)S(1)}, u32[]{:S(2)}, u32[]{:S(2)}) async-start(f32[32,1,2048]{2,1,0:T(1,128)} %reshape.44), calls=%async_computation.3 | async-start | bytes 524288 | tf_op jit(solution)/shard_map/all_to_all | solution.py:32
  81.2 4.1 %fusion.8 = f32[1024,256]{1,0:T(8,128)} fusion(bf16[1024,1024]{1,0:T(8,128)(2,1)S(1)} %copy-done, f32[256,1024]{1,0:T(8,128)} %param.7), kind=kOutput, calls=%fused_computation.20 | convolution fusion | flops 3221225472 | bytes 4194304 | tf_op jit(solution)/shard_map/dot_general | solution.py:70
  85.3 5.5 %all-to-all-done.3 = f32[32,1,2048]{2,1,0:T(1,128)S(1)} async-done(((f32[32,1,2048]{2,1,0:T(1,128)}), f32[32,1,2048]{2,1,0:T(1,128)S(1)}, u32[]{:S(2)}, u32[]{:S(2)}) %all-to-all-start.3) | async-done | bytes 262176 | tf_op jit(solution)/shard_map/all_to_all | solution.py:32
  90.8 0.7 copy-done.1
  91.5 16.1 %all-to-all-start.4 = ((f32[16,64,256]{2,1,0:T(8,128)}), f32[16,64,256]{2,1,0:T(8,128)}, u32[]{:S(2)}, u32[]{:S(2)}) async-start(f32[16,64,256]{2,1,0:T(8,128)} %bitcast.33), calls=%async_computation.4 | async-start | bytes 2097152 | tf_op jit(solution)/shard_map/all_to_all | solution.py:19
  107.6 2.2 %reduce.9 = f32[32,2048]{1,0:T(8,128)S(1)} reduce(f32[32,1,2048]{2,1,0:T(1,128)} %copy-done.1, f32[]{:T(128)} %broadcast.63), dimensions={1}, to_apply=%all_to_all.18.reduce_sub_computation | reduce | bytes 524292 | tf_op jit(solution)/shard_map/all_to_all | solution.py:32
  109.8 1.0 reshape.45
  110.8 1.1 broadcast_multiply_fusion
  111.9 3.6 %subtract_bitcast_fusion = (f32[1,256,1024]{2,1,0:T(8,128)}, f32[256,1024]{1,0:T(8,128)}) fusion(f32[256,1024]{1,0:T(8,128)S(1)} %fusion, f32[256,1024]{1,0:T(8,128)} %param.7, f32[64,256]{1,0:T(8,128)S(1)} %fusion.1, f32[1024,64]{1,0:T(8,128)S(1)} %bitcast.34), kind=kOutput, calls=%fused_computation.4 | convolution fusion | flops 201850880 | bytes 4521984 | tf_op jit(solution)/shard_map/dot_general | solution.py:67
  115.5 20.1 %all-to-all-done.4 = f32[16,64,256]{2,1,0:T(8,128)} async-done(((f32[16,64,256]{2,1,0:T(8,128)}), f32[16,64,256]{2,1,0:T(8,128)}, u32[]{:S(2)}, u32[]{:S(2)}) %all-to-all-start.4) | async-done | bytes 1048608 | tf_op jit(solution)/shard_map/all_to_all | solution.py:19
  135.7 1.9 %reduce_sum.29 = f32[64,256]{1,0:T(8,128)} reduce(f32[16,64,256]{2,1,0:T(8,128)} %all-to-all-done.4, f32[]{:T(128)} %constant.47.clone.1), dimensions={0}, to_apply=%region_4.5 | reduce | flops 245760 | bytes 1114116 | tf_op jit(solution)/shard_map/reduce_sum | solution.py:20
  (15 shorter events, 1.0 us)
Async XLA Ops:
  0.6 1.6 %copy-start = (bf16[1024,1024]{1,0:T(8,128)(2,1)S(1)}, bf16[1024,1024]{1,0:T(8,128)(2,1)}, u32[]{:S(2)}) copy-start(bf16[1024,1024]{1,0:T(8,128)(2,1)} %param.6) | copy-start | bytes 6291460
  0.6 3.7 %copy-start.2 = (f32[1024,64]{0,1:T(8,128)S(1)}, f32[1024,64]{0,1:T(8,128)}, u32[]{:S(2)}) copy-start(f32[1024,64]{0,1:T(8,128)} %param.9) | copy-start | bytes 786436
  76.8 14.0 %all-to-all-start.3 = ((f32[32,1,2048]{2,1,0:T(1,128)}), f32[32,1,2048]{2,1,0:T(1,128)S(1)}, u32[]{:S(2)}, u32[]{:S(2)}) async-start(f32[32,1,2048]{2,1,0:T(1,128)} %reshape.44), calls=%async_computation.3 | async-start | bytes 524288 | tf_op jit(solution)/shard_map/all_to_all | solution.py:32
  90.8 0.7 copy-start.1
  91.5 44.2 %all-to-all-start.4 = ((f32[16,64,256]{2,1,0:T(8,128)}), f32[16,64,256]{2,1,0:T(8,128)}, u32[]{:S(2)}, u32[]{:S(2)}) async-start(f32[16,64,256]{2,1,0:T(8,128)} %bitcast.33), calls=%async_computation.4 | async-start | bytes 2097152 | tf_op jit(solution)/shard_map/all_to_all | solution.py:19
where the time goes:
time: 138 us
  blocking collectives  44.6 us (32%)
  waiting for transfers between devices  25.7 us (19%)
  other arithmetic  22.3 us (16%)
  starting transfers between devices  20.4 us (15%)
  matrix products  14.2 us (10%)
  local copies, waits for them, and re-layouts  9.61 us (7%)
    all_to_all x2, blocking collectives, sum_at_owner(): lax.all_to_all(parts, axis, split_axis=0, concat_axis=0, tiled=True)  32.6 us
    all_to_all x1, waiting for transfers between devices, sum_at_owner(): lax.all_to_all(parts, axis, split_axis=0, concat_axis=0, tiled=True)  20.1 us
    all_to_all x1, starting transfers between devices, sum_at_owner(): lax.all_to_all(parts, axis, split_axis=0, concat_axis=0, tiled=True)  16.1 us
    all_to_all x1, blocking collectives, copy_for_each(): lax.all_to_all(jnp.broadcast_to(shard[None], (devices, *shard.shape)), ax...  12 us
    unnamed x14, local copies, waits for them, and re-layouts  8.16 us
    another operation x3, other arithmetic, local(): chol = jnp.linalg.cholesky(gram)  6.52 us
    another operation x2, other arithmetic, local(): ortho = jax.scipy.linalg.solve_triangular(chol, left.T, lower=True).T  5.55 us
    all_to_all x1, waiting for transfers between devices, copy_for_each(): lax.all_to_all(jnp.broadcast_to(shard[None], (devices, *shard.shape)), ax...  5.52 us
  transfers between devices with their start and end apart: 2, of which 2 were waited for; matrix products, arithmetic and copies ran while one was open for 9% of the time, Pallas kernels for 0%

commit v1 on v0

v1 whole, which is shorter than its diff:
```python
import functools

import jax
import jax.numpy as jnp
from jax import lax
from jax.experimental import pallas as pl
from jax.experimental.pallas import tpu as pltpu
from jax.sharding import PartitionSpec as P

HIGH = lax.Precision.HIGHEST
F32 = jnp.float32
BF16 = jnp.bfloat16
NN = (((1,), (0,)), ((), ()))
NT = (((1,), (1,)), ((), ()))

NX, NY = 4, 8
NDP = NX * NY
NZ = 8

DIN, COL, TOK, RANK = 256, 1024, 1024, 64
BLK = 256
NB = COL // BLK
ROWS = TOK // (2 * NZ)
TILES = 16


def split(x):
    hi = x.astype(BF16)
    lo = (x - hi.astype(F32)).astype(BF16)
    return hi, lo


def dot(a, b, dims=NN):
    return lax.dot_general(a, b, dims, preferred_element_type=F32)


def spd_inverse(a):
    n = a.shape[0]
    rows = lax.broadcasted_iota(jnp.int32, (n, n), 0)
    cols = lax.broadcasted_iota(jnp.int32, (n, n), 1)
    lane = lax.broadcasted_iota(jnp.int32, (1, n), 1)

    def sweep(k, a):
        at_row, at_col = rows == k, cols == k
        row = jnp.sum(jnp.where(at_row, a, 0.0), axis=0, keepdims=True)
        col = jnp.sum(jnp.where(at_col, a, 0.0), axis=1, keepdims=True)
        pivot = jnp.sum(jnp.where(lane == k, row, 0.0), axis=1, keepdims=True)
        inv = 1.0 / pivot
        scaled = row * inv
        out = a - col * scaled
        out = jnp.where(at_col, col * inv, out)
        return jnp.where(at_row, jnp.where(lane == k, -inv, scaled), out)

    return -lax.fori_loop(0, n, sweep, a)


def mixed(i, n):
    return n // 2 + (2 * lax.rem(i + 1, 2) - 1) * ((i + 1) // 2)


def by_parity(i, parity):
    even = 4 + (1 - 2 * lax.rem(i, 2)) * 2 * ((i + 1) // 2)
    odd = 4 + (2 * lax.rem(i, 2) - 1) * (2 * (i // 2) + 1)
    return even + parity * (odd - even)


def comm_kernel(
    acts_h, og_h, w_h, err_h, q_h,
    merged, b4, s_all, ig,
    acts_v, og_v, w_v, err_v, q_v,
    acts_t, mhi, mlo, qt, w_hi, w_lo,
    l_send, l_recv, l_all, s_send, s_recv, part, p_recv, psum, z_recv,
    load_sem, send_l, recv_l, send_la, recv_la, send_s, recv_s, send_sa, recv_sa,
    send_p, recv_p, send_z, recv_z,
):
    me = lax.axis_index("dp")
    x, y = me // NY, lax.rem(me, NY)
    t = lax.axis_index("tensor")
    z, core = t // 2, lax.rem(t, 2)

    loads = [
        pltpu.make_async_copy(q_h, q_v, load_sem.at[0]),
        pltpu.make_async_copy(acts_h, acts_v, load_sem.at[1]),
    ]
    for n in range(NB):
        at = pl.ds(n * BLK, BLK)
        loads.append(pltpu.make_async_copy(og_h.at[:, at], og_v.at[:, at], load_sem.at[2 + n]))
        loads.append(
            pltpu.make_async_copy(err_h.at[:, at], err_v.at[:, at], load_sem.at[2 + NB + n])
        )
    loads.append(pltpu.make_async_copy(w_h, w_v, load_sem.at[2 + 2 * NB]))
    for load in loads:
        load.start()

    def at_offset(i):
        return lax.rem(x + mixed(lax.rem(i, NX), NX), NX) * NY + lax.rem(
            y + mixed(i // NX, NY), NY
        )

    barrier = pltpu.get_barrier_semaphore()

    def greet(i, _):
        pl.semaphore_signal(
            barrier, inc=1, device_id={"dp": at_offset(i)}, device_id_type=pl.DeviceIdType.MESH
        )
        return _

    lax.fori_loop(0, NDP - 1, greet, 0)

    def greet_z(i, _):
        peer = lax.rem(z + mixed(i, NZ), NZ) * 2 + core
        pl.semaphore_signal(
            barrier, inc=1, device_id={"tensor": peer}, device_id_type=pl.DeviceIdType.MESH
        )
        return _

    lax.fori_loop(0, NZ - 1, greet_z, 0)
    partner = z * 2 + 1 - core
    pl.semaphore_signal(
        barrier, inc=1, device_id={"tensor": partner}, device_id_type=pl.DeviceIdType.MESH
    )

    loads[0].wait()
    q_hi, q_lo = split(q_v[...].T)
    qt[0:RANK, :] = q_hi
    qt[RANK:, :] = q_lo
    loads[1].wait()
    acts_t[...] = acts_v[...].T
    for n in range(NB):
        at = pl.ds(n * BLK, BLK)
        loads[2 + 2 * n].wait()
        loads[3 + 2 * n].wait()
        m = dot(acts_t[...], og_v[:, at]) * (TOK ** -0.5) + err_v[:, at]
        merged[:, at] = m
        hi, lo = split(m)
        mhi[:, at] = hi
        mlo[:, at] = lo
    both = dot(qt[...], mhi[...], NT)
    left = both[0:RANK] + both[RANK:] + dot(qt[0:RANK, :], mlo[...], NT)
    l_send[0:8] = left[:, 0:128].reshape(8, 8, 128)
    l_send[8:16] = left[:, 128:256].reshape(8, 8, 128)

    pl.semaphore_wait(barrier, NDP - 1 + NZ - 1 + 1)

    my_tile = x * 4 + y // 2
    owner = lax.rem(x + y, 2) == 0

    def left_copy(peer, tile):
        return pltpu.make_async_remote_copy(
            src_ref=l_send.at[tile], dst_ref=l_recv.at[me], send_sem=send_l, recv_sem=recv_l,
            device_id={"dp": peer}, device_id_type=pl.DeviceIdType.MESH,
        )

    def left_to(i, _):
        dx = mixed(lax.rem(i, NX), NX)
        px = lax.rem(x + dx, NX)
        parity = lax.rem(x + y + dx, 2)
        py = lax.rem(y + by_parity(i // NX, parity), NY)
        peer = px * NY + py
        tile = px * 4 + py // 2

        @pl.when(peer != me)
        def _():
            left_copy(peer, tile).start()

        return _

    def skip(i, _):
        left_to(i, 0)
        return _

    lax.fori_loop(0, TILES, skip, 0)

    @pl.when(owner)
    def _():
        l_recv[me] = l_send[my_tile]

    loads[2 + 2 * NB].wait()
    wh, wl = split(w_v[...])
    w_hi[...] = wh
    w_lo[...] = wl

    def part_rows(i, _):
        rows = og_v[pl.ds(pl.multiple_of(i * 256, 256), 256), :]
        p = dot(rows, w_hi[...], NT) + dot(rows, w_lo[...], NT)
        p = p.reshape(2, 2, ROWS, DIN)
        for c in range(2):
            for half in range(2):
                part[c, 2 * i + half] = p[half, c]
        return _

    lax.fori_loop(0, TOK // 256, part_rows, 0)
    to_partner = pltpu.make_async_remote_copy(
        src_ref=part.at[1 - core], dst_ref=p_recv, send_sem=send_p, recv_sem=recv_p,
        device_id={"tensor": partner}, device_id_type=pl.DeviceIdType.MESH,
    )
    to_partner.start()

    def left_all(peer):
        return pltpu.make_async_remote_copy(
            src_ref=l_all.at[my_tile], dst_ref=l_all.at[my_tile], send_sem=send_la,
            recv_sem=recv_la, device_id={"dp": peer}, device_id_type=pl.DeviceIdType.MESH,
        )

    @pl.when(owner)
    def _():
        pltpu.make_async_copy(
            l_recv.at[pl.ds(0, NDP - 1)], l_recv.at[pl.ds(0, NDP - 1)], recv_l
        ).wait()
        l_all[my_tile] = jnp.sum(l_recv[...], axis=0) * (1.0 / NDP)

        def to(i, _):
            left_all(at_offset(i)).start()
            return _

        lax.fori_loop(0, NDP - 1, to, 0)

    to_partner.wait_recv()

    def pair_sum(i, _):
        psum[i] = part[core, i] + p_recv[i]
        return _

    lax.fori_loop(0, NZ, pair_sum, 0)

    def z_copy(pz):
        return pltpu.make_async_remote_copy(
            src_ref=psum.at[pz], dst_ref=z_recv.at[z], send_sem=send_z, recv_sem=recv_z,
            device_id={"tensor": pz * 2 + core}, device_id_type=pl.DeviceIdType.MESH,
        )

    def z_to(i, _):
        z_copy(lax.rem(z + mixed(i, NZ), NZ)).start()
        return _

    lax.fori_loop(0, NZ - 1, z_to, 0)
    z_recv[z] = psum[z]

    @pl.when(owner)
    def _():
        pltpu.make_async_copy(
            l_all.at[pl.ds(0, TILES - 1)], l_all.at[pl.ds(0, TILES - 1)], recv_la
        ).wait()

    @pl.when(jnp.logical_not(owner))
    def _():
        pltpu.make_async_copy(l_all, l_all, recv_la).wait()

    left = jnp.concatenate(
        [l_all[0:8].reshape(RANK, 128), l_all[8:16].reshape(RANK, 128)], axis=1
    )
    l_hi, l_lo = split(left)
    l_both = jnp.concatenate([l_hi, l_lo], axis=0)
    for n in range(NB):
        at = pl.ds(n * BLK, BLK)
        both = dot(l_both, mhi[:, at])
        s = both[0:RANK] + both[RANK:] + dot(l_hi, mlo[:, at])
        s_send[8 * n : 8 * n + 8] = s.reshape(8, 8, BLK)

    def s_to(i, _):
        peer = at_offset(i)
        pltpu.make_async_remote_copy(
            src_ref=s_send.at[peer], dst_ref=s_recv.at[me], send_sem=send_s, recv_sem=recv_s,
            device_id={"dp": peer}, device_id_type=pl.DeviceIdType.MESH,
        ).start()
        return _

    lax.fori_loop(0, NDP - 1, s_to, 0)
    s_recv[me] = s_send[me]

    gram = lax.dot_general(left, left, NT, precision=HIGH, preferred_element_type=F32)
    inv = spd_inverse(gram)
    bt = lax.dot_general(inv, left, NN, precision=HIGH, preferred_element_type=F32)
    b_hi, b_lo = split(bt.T * (1.0 / NDP))
    b4[...] = jnp.concatenate([b_hi, b_hi, b_lo, b_lo], axis=1)

    pltpu.make_async_copy(
        s_recv.at[pl.ds(0, NDP - 1)], s_recv.at[pl.ds(0, NDP - 1)], recv_s
    ).wait()
    s_all[me] = jnp.sum(s_recv[...], axis=0)

    def s_all_to(i, _):
        pltpu.make_async_remote_copy(
            src_ref=s_all.at[me], dst_ref=s_all.at[me], send_sem=send_sa, recv_sem=recv_sa,
            device_id={"dp": at_offset(i)}, device_id_type=pl.DeviceIdType.MESH,
        ).start()
        return _

    lax.fori_loop(0, NDP - 1, s_all_to, 0)

    pltpu.make_async_copy(
        z_recv.at[pl.ds(0, NZ - 1)], z_recv.at[pl.ds(0, NZ - 1)], recv_z
    ).wait()
    ig[...] = jnp.sum(z_recv[...], axis=0)

    to_partner.wait_send()
    pltpu.make_async_copy(psum.at[pl.ds(0, NZ - 1)], psum.at[pl.ds(0, NZ - 1)], send_z).wait()

    @pl.when(owner)
    def _():
        pltpu.make_async_copy(
            l_send.at[pl.ds(0, TILES - 1)], l_send.at[pl.ds(0, TILES - 1)], send_l
        ).wait()
        pltpu.make_async_copy(
            l_recv.at[pl.ds(0, NDP - 1)], l_recv.at[pl.ds(0, NDP - 1)], send_la
        ).wait()

    @pl.when(jnp.logical_not(owner))
    def _():
        pltpu.make_async_copy(l_send, l_send, send_l).wait()

    for sem in (send_s, send_sa, recv_sa):
        pltpu.make_async_copy(
            s_send.at[pl.ds(0, NDP - 1)], s_send.at[pl.ds(0, NDP - 1)], sem
        ).wait()


def finish_kernel(merged, b4, s_all, w, ig_in, new_w, new_e, ig):
    s_hi, s_lo = split(s_all[...].reshape(RANK, BLK))
    delta = dot(b4[...], jnp.concatenate([s_hi, s_lo, s_hi, s_lo], axis=0))
    new_e[...] = merged[...] - delta
    new_w[...] = w[...] - delta

    @pl.when(pl.program_id(0) == 0)
    def _():
        ig[...] = ig_in[...]


def local(acts, out_grad, weight, error, start_q):
    hbm = pl.BlockSpec(memory_space=pl.ANY)
    vmem = pl.BlockSpec(memory_space=pltpu.VMEM)
    shape = jax.ShapeDtypeStruct
    dma = pltpu.SemaphoreType.DMA
    merged, b4, s_all, ig = pl.pallas_call(
        comm_kernel,
        out_shape=(
            shape((DIN, COL), F32),
            shape((DIN, 4 * RANK), BF16),
            shape((NDP, 8, BLK), F32),
            shape((ROWS, DIN), F32),
        ),
        in_specs=[hbm] * 5,
        out_specs=(vmem,) * 4,
        scratch_shapes=[
            pltpu.VMEM((TOK, DIN), BF16),
            pltpu.VMEM((TOK, COL), BF16),
            pltpu.VMEM((DIN, COL), F32),
            pltpu.VMEM((DIN, COL), F32),
            pltpu.VMEM((COL, RANK), F32),
            pltpu.VMEM((DIN, TOK), BF16),
            pltpu.VMEM((DIN, COL), BF16),
            pltpu.VMEM((DIN, COL), BF16),
            pltpu.VMEM((2 * RANK, COL), BF16),
            pltpu.VMEM((DIN, COL), BF16),
            pltpu.VMEM((DIN, COL), BF16),
            pltpu.VMEM((TILES, 8, 128), F32),
            pltpu.VMEM((NDP, 8, 128), F32),
            pltpu.VMEM((TILES, 8, 128), F32),
            pltpu.VMEM((NDP, 8, BLK), F32),
            pltpu.VMEM((NDP, 8, BLK), F32),
            pltpu.VMEM((2, NZ, ROWS, DIN), F32),
            pltpu.VMEM((NZ, ROWS, DIN), F32),
            pltpu.VMEM((NZ, ROWS, DIN), F32),
            pltpu.VMEM((NZ, ROWS, DIN), F32),
            dma((3 + 2 * NB,)),
        ]
        + [dma] * 12,
        compiler_params=pltpu.CompilerParams(
            collective_id=0, has_side_effects=True, vmem_limit_bytes=40 * 1024 * 1024
        ),
        name="powersgd_comm",
    )(acts, out_grad, weight, error[0], start_q)
    block = pl.BlockSpec((DIN, BLK), lambda n: (0, n))
    whole = pl.BlockSpec((ROWS, DIN), lambda n: (0, 0))
    new_weight, new_error, input_grad = pl.pallas_call(
        finish_kernel,
        grid=(NB,),
        out_shape=(shape((DIN, COL), F32), shape((DIN, COL), F32), shape((ROWS, DIN), F32)),
        in_specs=[
            block,
            pl.BlockSpec((DIN, 4 * RANK), lambda n: (0, 0)),
            pl.BlockSpec((8, 8, BLK), lambda n: (n, 0, 0)),
            block,
            whole,
        ],
        out_specs=(block, block, whole),
        name="powersgd_finish",
    )(merged, b4, s_all, weight, ig)
    return new_weight, new_error[None], input_grad


def solution(mesh):
    placed = (
        P("dp", None),
        P("dp", "tensor"),
        P(None, "tensor"),
        P("dp", None, "tensor"),
        P("tensor", None),
    )
    return jax.shard_map(
        local,
        mesh=mesh,
        in_specs=placed,
        out_specs=(P(None, "tensor"), P("dp", None, "tensor"), P(("dp", "tensor"), None)),
        check_vma=False,
    )
```

time: 138 us -> 57.1 us (0.41)
  the two profiles are of different devices: /device:TPU:1 before, /device:TPU:8 now
where the time goes in v1:
time: 57.1 us; the launch traced here: 56.7 us
  Pallas kernels  46.9 us (82%)
  local copies, waits for them, and re-layouts  9.15 us (16%)
  between operations  0.67 us (1%)
    pallas_call x1, Pallas kernels, local(): pl.pallas_call(comm_kernel, out_shape=(shape((DIN, COL), F32), shape((DIN...  42.7 us
    unnamed x17, local copies, waits for them, and re-layouts  9.15 us
    pallas_call x1, Pallas kernels, local(): pl.pallas_call(finish_kernel, grid=(NB,), out_shape=(shape((DIN, COL), F3...  4.22 us

profile of v1, /device:TPU:8, one launch (start us, length us, event | category | flops | bytes accessed | tf_op | source)
XLA Modules:
  0.0 56.7 jit_solution(52815184153164672)
XLA Ops:
  0.6 1.1 %copy.8.q_h = f32[1024,64]{1,0:T(8,128)S(1)} copy(f32[1024,64]{0,1:T(8,128)} %param.9) | data formatting | bytes 524288 | tf_op args[4]
  1.8 0.0 copy-start
  1.8 1.2 %copy-done = f32[256,1024]{1,0:T(8,128)S(1)} copy-done((f32[256,1024]{1,0:T(8,128)S(1)}, f32[256,1024]{1,0:T(8,128)}, u32[]{:S(2)}) %copy-start) | copy-done | bytes 1048600
  3.0 0.0 copy-start.1
  3.0 1.6 %copy-done.1 = bf16[1024,1024]{1,0:T(8,128)(2,1)S(1)} copy-done((bf16[1024,1024]{1,0:T(8,128)(2,1)S(1)}, bf16[1024,1024]{1,0:T(8,128)(2,1)}, u32[]{:S(2)}) %copy-start.1) | copy-done | bytes 2097176
  4.6 0.0 copy-start.2
  4.6 1.2 %copy-done.2 = f32[1,256,1024]{2,1,0:T(8,128)S(1)} copy-done((f32[1,256,1024]{2,1,0:T(8,128)S(1)}, f32[1,256,1024]{2,1,0:T(8,128)}, u32[]{:S(2)}) %copy-start.2) | copy-done | bytes 1048600
  5.8 0.0 copy-start.4
  5.8 1.0 %copy-done.4 = bf16[1024,256]{1,0:T(8,128)(2,1)S(1)} copy-done((bf16[1024,256]{1,0:T(8,128)(2,1)S(1)}, bf16[1024,256]{1,0:T(8,128)(2,1)}, u32[]{:S(2)}) %copy-start.4) | copy-done | bytes 524312
  6.9 42.7 %powersgd_comm.1 = (f32[256,1024]{1,0:T(8,128)S(1)}, bf16[256,256]{1,0:T(8,128)(2,1)S(1)}, f32[32,8,256]{2,1,0:T(8,128)S(1)}, f32[64,256]{1,0:T(8,128)S(1)}) custom-call(bf16[1024,256]{1,0:T(8,128)(2,1)S(1)} %copy-done.4, bf16[1024,1024]{1,0:T(8,128)(2,1)S(1)} %copy-done.1, f32[256,1024]{1,0:T(8,128)S(1)} %copy-done, f32[256,1024]{1,0:T(8,128)S(1)} %bitcast.2, ...), custom_call_target="tpu_custom_call" | custom-call | tf_op jit(solution)/shard_map/powersgd_comm/pallas_call | solution.py:334
  49.6 0.0 copy-start.3
  49.6 1.0 %copy-done.3 = f32[256,1024]{1,0:T(8,128)} copy-done((f32[256,1024]{1,0:T(8,128)}, f32[256,1024]{1,0:T(8,128)S(1)}, u32[]{:S(2)}) %copy-start.3) | copy-done | bytes 1048600
  50.5 0.0 copy-start.5
  50.5 0.7 %copy-done.5 = f32[32,8,256]{2,1,0:T(8,128)} copy-done((f32[32,8,256]{2,1,0:T(8,128)}, f32[32,8,256]{2,1,0:T(8,128)S(1)}, u32[]{:S(2)}) %copy-start.5) | copy-done | bytes 262168
  51.2 0.0 copy-start.6
  51.2 0.6 %copy-done.6 = bf16[256,256]{1,0:T(8,128)(2,1)} copy-done((bf16[256,256]{1,0:T(8,128)(2,1)}, bf16[256,256]{1,0:T(8,128)(2,1)S(1)}, u32[]{:S(2)}) %copy-start.6) | copy-done | bytes 131096
  51.9 0.0 copy-start.7
  51.9 0.6 %copy-done.7 = f32[64,256]{1,0:T(8,128)} copy-done((f32[64,256]{1,0:T(8,128)}, f32[64,256]{1,0:T(8,128)S(1)}, u32[]{:S(2)}) %copy-start.7) | copy-done | bytes 65560
  52.5 4.2 %powersgd_finish.1 = (f32[256,1024]{1,0:T(8,128)}, f32[256,1024]{1,0:T(8,128)}, f32[64,256]{1,0:T(8,128)}) custom-call(f32[256,1024]{1,0:T(8,128)} %copy-done.3, bf16[256,256]{1,0:T(8,128)(2,1)} %copy-done.6, f32[32,8,256]{2,1,0:T(8,128)} %copy-done.5, f32[256,1024]{1,0:T(8,128)} %w.1, f32[64,256]{1,0:T(8,128)} %copy-done.7), custom_call_target="tpu_custom_call" | custom-call | tf_op jit(solution)/shard_map/powersgd_finish/pallas_call | solution.py:375
Async XLA Ops:
  1.8 1.2 %copy-start = (f32[256,1024]{1,0:T(8,128)S(1)}, f32[256,1024]{1,0:T(8,128)}, u32[]{:S(2)}) copy-start(f32[256,1024]{1,0:T(8,128)} %w.1) | copy-start | bytes 3145732
  3.0 1.6 %copy-start.1 = (bf16[1024,1024]{1,0:T(8,128)(2,1)S(1)}, bf16[1024,1024]{1,0:T(8,128)(2,1)}, u32[]{:S(2)}) copy-start(bf16[1024,1024]{1,0:T(8,128)(2,1)} %og_h.1) | copy-start | bytes 6291460
  4.6 1.2 %copy-start.2 = (f32[1,256,1024]{2,1,0:T(8,128)S(1)}, f32[1,256,1024]{2,1,0:T(8,128)}, u32[]{:S(2)}) copy-start(f32[1,256,1024]{2,1,0:T(8,128)} %param.8) | copy-start | bytes 3145732
  5.8 1.0 %copy-start.4 = (bf16[1024,256]{1,0:T(8,128)(2,1)S(1)}, bf16[1024,256]{1,0:T(8,128)(2,1)}, u32[]{:S(2)}) copy-start(bf16[1024,256]{1,0:T(8,128)(2,1)} %acts_h.1) | copy-start | bytes 1572868
  49.6 1.0 %copy-start.3 = (f32[256,1024]{1,0:T(8,128)}, f32[256,1024]{1,0:T(8,128)S(1)}, u32[]{:S(2)}) copy-start(f32[256,1024]{1,0:T(8,128)S(1)} %get-tuple-element.10.merged) | copy-start | bytes 3145732
  50.5 0.7 %copy-start.5 = (f32[32,8,256]{2,1,0:T(8,128)}, f32[32,8,256]{2,1,0:T(8,128)S(1)}, u32[]{:S(2)}) copy-start(f32[32,8,256]{2,1,0:T(8,128)S(1)} %get-tuple-element.12.s_all) | copy-start | bytes 786436
  51.2 0.6 %copy-start.6 = (bf16[256,256]{1,0:T(8,128)(2,1)}, bf16[256,256]{1,0:T(8,128)(2,1)S(1)}, u32[]{:S(2)}) copy-start(bf16[256,256]{1,0:T(8,128)(2,1)S(1)} %get-tuple-element.11.b4) | copy-start | bytes 393220
  51.9 0.6 %copy-start.7 = (f32[64,256]{1,0:T(8,128)}, f32[64,256]{1,0:T(8,128)S(1)}, u32[]{:S(2)}) copy-start(f32[64,256]{1,0:T(8,128)S(1)} %get-tuple-element.13.ig_in) | copy-start | bytes 196612

commit v2 on v1

--- a/solution.py
+++ b/solution.py
@@ -66,8 +66,8 @@
 
 def comm_kernel(
     acts_h, og_h, w_h, err_h, q_h,
-    merged, b4, s_all, ig,
-    acts_v, og_v, w_v, err_v, q_v,
+    merged, b4, s_all, ig, w_v,
+    acts_v, og_v, err_v, q_v,
     acts_t, mhi, mlo, qt, w_hi, w_lo,
     l_send, l_recv, l_all, s_send, s_recv, part, p_recv, psum, z_recv,
     load_sem, send_l, recv_l, send_la, recv_la, send_s, recv_s, send_sa, recv_sa,
@@ -121,7 +121,7 @@
     )
 
     loads[0].wait()
-    q_hi, q_lo = split(q_v[...].T)
+    q_hi, q_lo = split(q_v[...])
     qt[0:RANK, :] = q_hi
     qt[RANK:, :] = q_lo
     loads[1].wait()
@@ -315,38 +315,45 @@
         ).wait()
 
 
-def finish_kernel(merged, b4, s_all, w, ig_in, new_w, new_e, ig):
-    s_hi, s_lo = split(s_all[...].reshape(RANK, BLK))
-    delta = dot(b4[...], jnp.concatenate([s_hi, s_lo, s_hi, s_lo], axis=0))
-    new_e[...] = merged[...] - delta
-    new_w[...] = w[...] - delta
-
-    @pl.when(pl.program_id(0) == 0)
-    def _():
-        ig[...] = ig_in[...]
+def finish_kernel(merged, b4, s_all, w, ig_in, new_w, new_e, ig, w_v, e_v, out_sem):
+    copies = [pltpu.make_async_copy(ig_in, ig, out_sem.at[0])]
+    copies[0].start()
+    for n in range(NB):
+        at = pl.ds(n * BLK, BLK)
+        s_hi, s_lo = split(s_all[8 * n : 8 * n + 8].reshape(RANK, BLK))
+        delta = dot(b4[...], jnp.concatenate([s_hi, s_lo, s_hi, s_lo], axis=0))
+        e_v[:, at] = merged[:, at] - delta
+        w_v[:, at] = w[:, at] - delta
+        for i, (src, dst) in enumerate(((e_v, new_e), (w_v, new_w))):
+            copies.append(
+                pltpu.make_async_copy(src.at[:, at], dst.at[:, at], out_sem.at[1 + 2 * n + i])
+            )
+            copies[-1].start()
+    for copy in copies:
+        copy.wait()
 
 
 def local(acts, out_grad, weight, error, start_q):
-    hbm = pl.BlockSpec(memory_space=pl.ANY)
+    hbm = pl.BlockSpec(memory_space=pltpu.HBM)
     vmem = pl.BlockSpec(memory_space=pltpu.VMEM)
     shape = jax.ShapeDtypeStruct
     dma = pltpu.SemaphoreType.DMA
-    merged, b4, s_all, ig = pl.pallas_call(
+    merged, b4, s_all, ig, weight_v = pl.pallas_call(
         comm_kernel,
         out_shape=(
             shape((DIN, COL), F32),
             shape((DIN, 4 * RANK), BF16),
             shape((NDP, 8, BLK), F32),
             shape((ROWS, DIN), F32),
+            shape((DIN, COL), F32),
         ),
         in_specs=[hbm] * 5,
-        out_specs=(vmem,) * 4,
+        out_specs=(vmem,) * 5,
         scratch_shapes=[
             pltpu.VMEM((TOK, DIN), BF16),
             pltpu.VMEM((TOK, COL), BF16),
             pltpu.VMEM((DIN, COL), F32),
-            pltpu.VMEM((DIN, COL), F32),
-            pltpu.VMEM((COL, RANK), F32),
+            pltpu.VMEM((RANK, COL), F32),
             pltpu.VMEM((DIN, TOK), BF16),
             pltpu.VMEM((DIN, COL), BF16),
             pltpu.VMEM((DIN, COL), BF16),
@@ -369,23 +376,20 @@
             collective_id=0, has_side_effects=True, vmem_limit_bytes=40 * 1024 * 1024
         ),
         name="powersgd_comm",
-    )(acts, out_grad, weight, error[0], start_q)
-    block = pl.BlockSpec((DIN, BLK), lambda n: (0, n))
-    whole = pl.BlockSpec((ROWS, DIN), lambda n: (0, 0))
+    )(*(pltpu.with_memory_space_constraint(a, pltpu.HBM) for a in (acts, out_grad, weight, error[0], start_q.T)))
     new_weight, new_error, input_grad = pl.pallas_call(
         finish_kernel,
-        grid=(NB,),
         out_shape=(shape((DIN, COL), F32), shape((DIN, COL), F32), shape((ROWS, DIN), F32)),
-        in_specs=[
-            block,
-            pl.BlockSpec((DIN, 4 * RANK), lambda n: (0, 0)),
-            pl.BlockSpec((8, 8, BLK), lambda n: (n, 0, 0)),
-            block,
-            whole,
+        in_specs=[vmem] * 5,
+        out_specs=(hbm,) * 3,
+        scratch_shapes=[
+            pltpu.VMEM((DIN, COL), F32),
+            pltpu.VMEM((DIN, COL), F32),
+            dma((1 + 2 * NB,)),
         ],
-        out_specs=(block, block, whole),
+        compiler_params=pltpu.CompilerParams(vmem_limit_bytes=16 * 1024 * 1024),
         name="powersgd_finish",
-    )(merged, b4, s_all, weight, ig)
+    )(merged, b4, s_all, weight_v, ig)
     return new_weight, new_error[None], input_grad
 
 

time: 57.1 us -> 44.6 us (0.78)
  local copies, waits for them, and re-layouts: 9.15 us -> 0 us
  Pallas kernels: 46.9 us -> 43.9 us
    unnamed x17 -> x0, local copies, waits for them, and re-layouts: 9.15 us -> none
    pallas_call x1, Pallas kernels: 4.22 us -> 1.64 us  [local(): pl.pallas_call(finish_kernel, out_shape=(shape((DIN, COL), F32), shape((D...]
where the time goes in v2:
time: 44.6 us; the launch traced here: 44.5 us
  Pallas kernels  43.9 us (98%)
  between operations  0.64 us (1%)
    pallas_call x1, Pallas kernels, local(): pl.pallas_call(comm_kernel, out_shape=(shape((DIN, COL), F32), shape((DIN...  42.2 us
    pallas_call x1, Pallas kernels, local(): pl.pallas_call(finish_kernel, out_shape=(shape((DIN, COL), F32), shape((D...  1.64 us

profile of v2, /device:TPU:8, one launch (start us, length us, event | category | flops | bytes accessed | tf_op | source)
XLA Modules:
  0.0 44.5 jit_solution(12605729168186852496)
XLA Ops:
  0.6 42.2 %powersgd_comm.1 = (f32[256,1024]{1,0:T(8,128)S(1)}, bf16[256,256]{1,0:T(8,128)(2,1)S(1)}, f32[32,8,256]{2,1,0:T(8,128)S(1)}, f32[64,256]{1,0:T(8,128)S(1)}, f32[256,1024]{1,0:T(8,128)S(1)}) custom-call(bf16[1024,256]{1,0:T(8,128)(2,1)} %acts_h.1, bf16[1024,1024]{1,0:T(8,128)(2,1)} %og_h.1, f32[256,1024]{1,0:T(8,128)} %w_h.1, f32[256,1024]{1,0:T(8,128)} %bitcast.3, ...), custom_call_target="tpu_custom_call" | custom-call | tf_op jit(solution)/shard_map/powersgd_comm/pallas_call | solution.py:341
  42.9 1.6 %powersgd_finish.1 = (f32[256,1024]{1,0:T(8,128)}, f32[256,1024]{1,0:T(8,128)}, f32[64,256]{1,0:T(8,128)}) custom-call(f32[256,1024]{1,0:T(8,128)S(1)} %get-tuple-element.11.merged, bf16[256,256]{1,0:T(8,128)(2,1)S(1)} %get-tuple-element.12.b4, f32[32,8,256]{2,1,0:T(8,128)S(1)} %get-tuple-element.13.s_all, f32[256,1024]{1,0:T(8,128)S(1)} %get-tuple-element.14.w, ...), custom_call_target="tpu_custom_call" | custom-call | tf_op jit(solution)/shard_map/powersgd_finish/pallas_call | solution.py:380

commit v3 on v2

--- a/solution.py
+++ b/solution.py
@@ -34,7 +34,7 @@
     return lax.dot_general(a, b, dims, preferred_element_type=F32)
 
 
-def spd_inverse(a):
+def sweeps(a, start, stop):
     n = a.shape[0]
     rows = lax.broadcasted_iota(jnp.int32, (n, n), 0)
     cols = lax.broadcasted_iota(jnp.int32, (n, n), 1)
@@ -51,17 +51,13 @@
         out = jnp.where(at_col, col * inv, out)
         return jnp.where(at_row, jnp.where(lane == k, -inv, scaled), out)
 
-    return -lax.fori_loop(0, n, sweep, a)
-
-
-def mixed(i, n):
-    return n // 2 + (2 * lax.rem(i + 1, 2) - 1) * ((i + 1) // 2)
-
-
-def by_parity(i, parity):
-    even = 4 + (1 - 2 * lax.rem(i, 2)) * 2 * ((i + 1) // 2)
-    odd = 4 + (2 * lax.rem(i, 2) - 1) * (2 * (i // 2) + 1)
-    return even + parity * (odd - even)
+    return lax.fori_loop(start, stop, sweep, a)
+
+
+FAR_X = (2, 1, 3, 0)
+FAR_Y = (4, 3, 5, 2, 6, 1, 7, 0)
+FAR_EVEN, FAR_ODD = (4, 2, 6, 0), (3, 5, 1, 7)
+HALF = 36
 
 
 def comm_kernel(
@@ -92,33 +88,19 @@
     for load in loads:
         load.start()
 
-    def at_offset(i):
-        return lax.rem(x + mixed(lax.rem(i, NX), NX), NX) * NY + lax.rem(
-            y + mixed(i // NX, NY), NY
-        )
+    xs = [lax.rem(x + d, NX) if d else x for d in FAR_X]
+    ys = [lax.rem(y + d, NY) if d else y for d in FAR_Y]
+    zs = [lax.rem(z + d, NZ) for d in FAR_Y[:-1]]
+    peers = [px * NY + py for py in ys for px in xs][:-1]
+    partner = z * 2 + 1 - core
 
     barrier = pltpu.get_barrier_semaphore()
-
-    def greet(i, _):
+    met = [{"dp": p} for p in peers] + [{"tensor": pz * 2 + core} for pz in zs]
+    met.append({"tensor": partner})
+    for device in met:
         pl.semaphore_signal(
-            barrier, inc=1, device_id={"dp": at_offset(i)}, device_id_type=pl.DeviceIdType.MESH
-        )
-        return _
-
-    lax.fori_loop(0, NDP - 1, greet, 0)
-
-    def greet_z(i, _):
-        peer = lax.rem(z + mixed(i, NZ), NZ) * 2 + core
-        pl.semaphore_signal(
-            barrier, inc=1, device_id={"tensor": peer}, device_id_type=pl.DeviceIdType.MESH
-        )
-        return _
-
-    lax.fori_loop(0, NZ - 1, greet_z, 0)
-    partner = z * 2 + 1 - core
-    pl.semaphore_signal(
-        barrier, inc=1, device_id={"tensor": partner}, device_id_type=pl.DeviceIdType.MESH
-    )
+            barrier, inc=1, device_id=device, device_id_type=pl.DeviceIdType.MESH
+        )
 
     loads[0].wait()
     q_hi, q_lo = split(q_v[...])
@@ -126,6 +108,8 @@
     qt[RANK:, :] = q_lo
     loads[1].wait()
     acts_t[...] = acts_v[...].T
+    both = jnp.zeros((2 * RANK, DIN), F32)
+    left = jnp.zeros((RANK, DIN), F32)
     for n in range(NB):
         at = pl.ds(n * BLK, BLK)
         loads[2 + 2 * n].wait()
@@ -135,12 +119,13 @@
         hi, lo = split(m)
         mhi[:, at] = hi
         mlo[:, at] = lo
-    both = dot(qt[...], mhi[...], NT)
-    left = both[0:RANK] + both[RANK:] + dot(qt[0:RANK, :], mlo[...], NT)
+        both += dot(qt[:, at], hi, NT)
+        left += dot(qt[0:RANK, at], lo, NT)
+    left += both[0:RANK] + both[RANK:]
     l_send[0:8] = left[:, 0:128].reshape(8, 8, 128)
     l_send[8:16] = left[:, 128:256].reshape(8, 8, 128)
 
-    pl.semaphore_wait(barrier, NDP - 1 + NZ - 1 + 1)
+    pl.semaphore_wait(barrier, len(met))
 
     my_tile = x * 4 + y // 2
     owner = lax.rem(x + y, 2) == 0
@@ -151,25 +136,17 @@
             device_id={"dp": peer}, device_id_type=pl.DeviceIdType.MESH,
         )
 
-    def left_to(i, _):
-        dx = mixed(lax.rem(i, NX), NX)
-        px = lax.rem(x + dx, NX)
-        parity = lax.rem(x + y + dx, 2)
-        py = lax.rem(y + by_parity(i // NX, parity), NY)
-        peer = px * NY + py
-        tile = px * 4 + py // 2
-
-        @pl.when(peer != me)
-        def _():
-            left_copy(peer, tile).start()
-
-        return _
-
-    def skip(i, _):
-        left_to(i, 0)
-        return _
-
-    lax.fori_loop(0, TILES, skip, 0)
+    odd = lax.rem(x + y, 2)
+    same = [lax.rem(y + e + odd * (o - e), NY) for e, o in zip(FAR_EVEN, FAR_ODD)]
+    other = [lax.rem(y + o + odd * (e - o), NY) for e, o in zip(FAR_EVEN, FAR_ODD)]
+    for j in range(4):
+        for dx, px in zip(FAR_X, xs):
+            py = (other if dx % 2 else same)[j]
+            copy = left_copy(px * NY + py, px * 4 + py // 2)
+            if dx == 0 and j == 3:
+                pl.when(jnp.logical_not(owner))(copy.start)
+            else:
+                copy.start()
 
     @pl.when(owner)
     def _():
@@ -209,11 +186,8 @@
         ).wait()
         l_all[my_tile] = jnp.sum(l_recv[...], axis=0) * (1.0 / NDP)
 
-        def to(i, _):
-            left_all(at_offset(i)).start()
-            return _
-
-        lax.fori_loop(0, NDP - 1, to, 0)
+        for peer in peers:
+            left_all(peer).start()
 
     to_partner.wait_recv()
 
@@ -229,11 +203,8 @@
             device_id={"tensor": pz * 2 + core}, device_id_type=pl.DeviceIdType.MESH,
         )
 
-    def z_to(i, _):
-        z_copy(lax.rem(z + mixed(i, NZ), NZ)).start()
-        return _
-
-    lax.fori_loop(0, NZ - 1, z_to, 0)
+    for pz in zs:
+        z_copy(pz).start()
     z_recv[z] = psum[z]
 
     @pl.when(owner)
@@ -251,42 +222,39 @@
     )
     l_hi, l_lo = split(left)
     l_both = jnp.concatenate([l_hi, l_lo], axis=0)
-    for n in range(NB):
-        at = pl.ds(n * BLK, BLK)
+    for dx, px in zip(FAR_X, xs):
+        at = pl.ds(pl.multiple_of(px * BLK, BLK), BLK)
         both = dot(l_both, mhi[:, at])
         s = both[0:RANK] + both[RANK:] + dot(l_hi, mlo[:, at])
-        s_send[8 * n : 8 * n + 8] = s.reshape(8, 8, BLK)
-
-    def s_to(i, _):
-        peer = at_offset(i)
-        pltpu.make_async_remote_copy(
-            src_ref=s_send.at[peer], dst_ref=s_recv.at[me], send_sem=send_s, recv_sem=recv_s,
-            device_id={"dp": peer}, device_id_type=pl.DeviceIdType.MESH,
-        ).start()
-        return _
-
-    lax.fori_loop(0, NDP - 1, s_to, 0)
+        s_send[pl.ds(px * NY, NY)] = s.reshape(NY, 8, BLK)
+        for dy, py in zip(FAR_Y, ys):
+            if dx or dy:
+                peer = px * NY + py
+                pltpu.make_async_remote_copy(
+                    src_ref=s_send.at[peer], dst_ref=s_recv.at[me], send_sem=send_s,
+                    recv_sem=recv_s, device_id={"dp": peer},
+                    device_id_type=pl.DeviceIdType.MESH,
+                ).start()
     s_recv[me] = s_send[me]
 
     gram = lax.dot_general(left, left, NT, precision=HIGH, preferred_element_type=F32)
-    inv = spd_inverse(gram)
-    bt = lax.dot_general(inv, left, NN, precision=HIGH, preferred_element_type=F32)
-    b_hi, b_lo = split(bt.T * (1.0 / NDP))
-    b4[...] = jnp.concatenate([b_hi, b_hi, b_lo, b_lo], axis=1)
+    swept = sweeps(gram, 0, HALF)
 
     pltpu.make_async_copy(
         s_recv.at[pl.ds(0, NDP - 1)], s_recv.at[pl.ds(0, NDP - 1)], recv_s
     ).wait()
     s_all[me] = jnp.sum(s_recv[...], axis=0)
 
-    def s_all_to(i, _):
+    for peer in peers:
         pltpu.make_async_remote_copy(
             src_ref=s_all.at[me], dst_ref=s_all.at[me], send_sem=send_sa, recv_sem=recv_sa,
-            device_id={"dp": at_offset(i)}, device_id_type=pl.DeviceIdType.MESH,
+            device_id={"dp": peer}, device_id_type=pl.DeviceIdType.MESH,
         ).start()
-        return _
-
-    lax.fori_loop(0, NDP - 1, s_all_to, 0)
+
+    inv = -sweeps(swept, HALF, RANK)
+    bt = lax.dot_general(inv, left, NN, precision=HIGH, preferred_element_type=F32)
+    b_hi, b_lo = split(bt.T * (1.0 / NDP))
+    b4[...] = jnp.concatenate([b_hi, b_hi, b_lo, b_lo], axis=1)
 
     pltpu.make_async_copy(
         z_recv.at[pl.ds(0, NZ - 1)], z_recv.at[pl.ds(0, NZ - 1)], recv_z

time: 44.6 us -> 41.4 us (0.928)
  Pallas kernels: 43.9 us -> 40.7 us
    pallas_call x1, Pallas kernels: 42.2 us -> 39 us  [local(): pl.pallas_call(comm_kernel, out_shape=(shape((DIN, COL), F32), shape((DIN...]
where the time goes in v3:
time: 41.4 us; the launch traced here: 41.3 us
  Pallas kernels  40.7 us (98%)
  between operations  0.64 us (2%)
    pallas_call x1, Pallas kernels, local(): pl.pallas_call(comm_kernel, out_shape=(shape((DIN, COL), F32), shape((DIN...  39 us
    pallas_call x1, Pallas kernels, local(): pl.pallas_call(finish_kernel, out_shape=(shape((DIN, COL), F32), shape((D...  1.64 us

profile of v3, /device:TPU:8, one launch (start us, length us, event | category | flops | bytes accessed | tf_op | source)
XLA Modules:
  0.0 41.3 jit_solution(2705240524816185856)
XLA Ops:
  0.6 39.0 %powersgd_comm.1 = (f32[256,1024]{1,0:T(8,128)S(1)}, bf16[256,256]{1,0:T(8,128)(2,1)S(1)}, f32[32,8,256]{2,1,0:T(8,128)S(1)}, f32[64,256]{1,0:T(8,128)S(1)}, f32[256,1024]{1,0:T(8,128)S(1)}) custom-call(bf16[1024,256]{1,0:T(8,128)(2,1)} %acts_h.1, bf16[1024,1024]{1,0:T(8,128)(2,1)} %og_h.1, f32[256,1024]{1,0:T(8,128)} %w_h.1, f32[256,1024]{1,0:T(8,128)} %bitcast.3, ...), custom_call_target="tpu_custom_call" | custom-call | tf_op jit(solution)/shard_map/powersgd_comm/pallas_call | solution.py:309
  39.7 1.6 %powersgd_finish.1 = (f32[256,1024]{1,0:T(8,128)}, f32[256,1024]{1,0:T(8,128)}, f32[64,256]{1,0:T(8,128)}) custom-call(f32[256,1024]{1,0:T(8,128)S(1)} %get-tuple-element.11.merged, bf16[256,256]{1,0:T(8,128)(2,1)S(1)} %get-tuple-element.12.b4, f32[32,8,256]{2,1,0:T(8,128)S(1)} %get-tuple-element.13.s_all, f32[256,1024]{1,0:T(8,128)S(1)} %get-tuple-element.14.w, ...), custom_call_target="tpu_custom_call" | custom-call | tf_op jit(solution)/shard_map/powersgd_finish/pallas_call | solution.py:348

commit v4 on v3

--- a/solution.py
+++ b/solution.py
@@ -19,7 +19,8 @@
 
 DIN, COL, TOK, RANK = 256, 1024, 1024, 64
 BLK = 256
-NB = COL // BLK
+LB = 2
+WIDE = COL // LB
 ROWS = TOK // (2 * NZ)
 TILES = 16
 
@@ -62,8 +63,8 @@
 
 def comm_kernel(
     acts_h, og_h, w_h, err_h, q_h,
-    merged, b4, s_all, ig, w_v,
-    acts_v, og_v, err_v, q_v,
+    new_e, new_w, ig,
+    merged, b4, s_all, w_v, acts_v, og_v, err_v, q_v,
     acts_t, mhi, mlo, qt, w_hi, w_lo,
     l_send, l_recv, l_all, s_send, s_recv, part, p_recv, psum, z_recv,
     load_sem, send_l, recv_l, send_la, recv_la, send_s, recv_s, send_sa, recv_sa,
@@ -78,13 +79,13 @@
         pltpu.make_async_copy(q_h, q_v, load_sem.at[0]),
         pltpu.make_async_copy(acts_h, acts_v, load_sem.at[1]),
     ]
-    for n in range(NB):
-        at = pl.ds(n * BLK, BLK)
+    for n in range(LB):
+        at = pl.ds(n * WIDE, WIDE)
         loads.append(pltpu.make_async_copy(og_h.at[:, at], og_v.at[:, at], load_sem.at[2 + n]))
         loads.append(
-            pltpu.make_async_copy(err_h.at[:, at], err_v.at[:, at], load_sem.at[2 + NB + n])
-        )
-    loads.append(pltpu.make_async_copy(w_h, w_v, load_sem.at[2 + 2 * NB]))
+            pltpu.make_async_copy(err_h.at[:, at], err_v.at[:, at], load_sem.at[2 + LB + n])
+        )
+    loads.append(pltpu.make_async_copy(w_h, w_v, load_sem.at[2 + 2 * LB]))
     for load in loads:
         load.start()
 
@@ -110,8 +111,8 @@
     acts_t[...] = acts_v[...].T
     both = jnp.zeros((2 * RANK, DIN), F32)
     left = jnp.zeros((RANK, DIN), F32)
-    for n in range(NB):
-        at = pl.ds(n * BLK, BLK)
+    for n in range(LB):
+        at = pl.ds(n * WIDE, WIDE)
         loads[2 + 2 * n].wait()
         loads[3 + 2 * n].wait()
         m = dot(acts_t[...], og_v[:, at]) * (TOK ** -0.5) + err_v[:, at]
@@ -152,7 +153,7 @@
     def _():
         l_recv[me] = l_send[my_tile]
 
-    loads[2 + 2 * NB].wait()
+    loads[2 + 2 * LB].wait()
     wh, wl = split(w_v[...])
     w_hi[...] = wh
     w_lo[...] = wl
@@ -247,8 +248,8 @@
 
     for peer in peers:
         pltpu.make_async_remote_copy(
-            src_ref=s_all.at[me], dst_ref=s_all.at[me], send_sem=send_sa, recv_sem=recv_sa,
-            device_id={"dp": peer}, device_id_type=pl.DeviceIdType.MESH,
+            src_ref=s_all.at[me], dst_ref=s_all.at[me], send_sem=send_sa,
+            recv_sem=recv_sa.at[x], device_id={"dp": peer}, device_id_type=pl.DeviceIdType.MESH,
         ).start()
 
     inv = -sweeps(swept, HALF, RANK)
@@ -261,6 +262,15 @@
     ).wait()
     ig[...] = jnp.sum(z_recv[...], axis=0)
 
+    for dx, px in reversed(tuple(zip(FAR_X, xs))):
+        arrived = s_recv.at[pl.ds(0, NY if dx else NY - 1)]
+        pltpu.make_async_copy(arrived, arrived, recv_sa.at[px]).wait()
+        at = pl.ds(pl.multiple_of(px * BLK, BLK), BLK)
+        s_hi, s_lo = split(s_all[pl.ds(px * NY, NY)].reshape(RANK, BLK))
+        delta = dot(b4[...], jnp.concatenate([s_hi, s_lo, s_hi, s_lo], axis=0))
+        new_e[:, at] = merged[:, at] - delta
+        new_w[:, at] = w_v[:, at] - delta
+
     to_partner.wait_send()
     pltpu.make_async_copy(psum.at[pl.ds(0, NZ - 1)], psum.at[pl.ds(0, NZ - 1)], send_z).wait()
 
@@ -277,26 +287,23 @@
     def _():
         pltpu.make_async_copy(l_send, l_send, send_l).wait()
 
-    for sem in (send_s, send_sa, recv_sa):
+    for sem in (send_s, send_sa):
         pltpu.make_async_copy(
             s_send.at[pl.ds(0, NDP - 1)], s_send.at[pl.ds(0, NDP - 1)], sem
         ).wait()
 
 
-def finish_kernel(merged, b4, s_all, w, ig_in, new_w, new_e, ig, w_v, e_v, out_sem):
-    copies = [pltpu.make_async_copy(ig_in, ig, out_sem.at[0])]
-    copies[0].start()
-    for n in range(NB):
-        at = pl.ds(n * BLK, BLK)
-        s_hi, s_lo = split(s_all[8 * n : 8 * n + 8].reshape(RANK, BLK))
-        delta = dot(b4[...], jnp.concatenate([s_hi, s_lo, s_hi, s_lo], axis=0))
-        e_v[:, at] = merged[:, at] - delta
-        w_v[:, at] = w[:, at] - delta
-        for i, (src, dst) in enumerate(((e_v, new_e), (w_v, new_w))):
+def finish_kernel(e_v, w_v, ig_v, new_e, new_w, ig, out_sem):
+    copies = []
+    for src, dst in ((e_v, new_e), (w_v, new_w)):
+        for half in range(2):
+            at = pl.ds(half * (DIN // 2), DIN // 2)
             copies.append(
-                pltpu.make_async_copy(src.at[:, at], dst.at[:, at], out_sem.at[1 + 2 * n + i])
+                pltpu.make_async_copy(src.at[at, :], dst.at[at, :], out_sem.at[len(copies)])
             )
-            copies[-1].start()
+    copies.append(pltpu.make_async_copy(ig_v, ig, out_sem.at[len(copies)]))
+    for copy in copies:
+        copy.start()
     for copy in copies:
         copy.wait()
 
@@ -306,18 +313,20 @@
     vmem = pl.BlockSpec(memory_space=pltpu.VMEM)
     shape = jax.ShapeDtypeStruct
     dma = pltpu.SemaphoreType.DMA
-    merged, b4, s_all, ig, weight_v = pl.pallas_call(
+    error_v, weight_v, ig = pl.pallas_call(
         comm_kernel,
         out_shape=(
             shape((DIN, COL), F32),
-            shape((DIN, 4 * RANK), BF16),
-            shape((NDP, 8, BLK), F32),
+            shape((DIN, COL), F32),
             shape((ROWS, DIN), F32),
-            shape((DIN, COL), F32),
         ),
         in_specs=[hbm] * 5,
-        out_specs=(vmem,) * 5,
+        out_specs=(vmem,) * 3,
         scratch_shapes=[
+            pltpu.VMEM((DIN, COL), F32),
+            pltpu.VMEM((DIN, 4 * RANK), BF16),
+            pltpu.VMEM((NDP, 8, BLK), F32),
+            pltpu.VMEM((DIN, COL), F32),
             pltpu.VMEM((TOK, DIN), BF16),
             pltpu.VMEM((TOK, COL), BF16),
             pltpu.VMEM((DIN, COL), F32),
@@ -337,27 +346,25 @@
             pltpu.VMEM((NZ, ROWS, DIN), F32),
             pltpu.VMEM((NZ, ROWS, DIN), F32),
             pltpu.VMEM((NZ, ROWS, DIN), F32),
-            dma((3 + 2 * NB,)),
+            dma((3 + 2 * LB,)),
         ]
-        + [dma] * 12,
+        + [dma] * 7
+        + [dma((NX,))]
+        + [dma] * 4,
         compiler_params=pltpu.CompilerParams(
             collective_id=0, has_side_effects=True, vmem_limit_bytes=40 * 1024 * 1024
         ),
         name="powersgd_comm",
     )(*(pltpu.with_memory_space_constraint(a, pltpu.HBM) for a in (acts, out_grad, weight, error[0], start_q.T)))
-    new_weight, new_error, input_grad = pl.pallas_call(
+    new_error, new_weight, input_grad = pl.pallas_call(
         finish_kernel,
         out_shape=(shape((DIN, COL), F32), shape((DIN, COL), F32), shape((ROWS, DIN), F32)),
-        in_specs=[vmem] * 5,
+        in_specs=[vmem] * 3,
         out_specs=(hbm,) * 3,
-        scratch_shapes=[
-            pltpu.VMEM((DIN, COL), F32),
-            pltpu.VMEM((DIN, COL), F32),
-            dma((1 + 2 * NB,)),
-        ],
+        scratch_shapes=[dma((5,))],
         compiler_params=pltpu.CompilerParams(vmem_limit_bytes=16 * 1024 * 1024),
         name="powersgd_finish",
-    )(merged, b4, s_all, weight_v, ig)
+    )(error_v, weight_v, ig)
     return new_weight, new_error[None], input_grad
 
 

time: 41.4 us -> 41.8 us (level)
    pallas_call x1, Pallas kernels: 39 us -> 39.7 us  [local(): pl.pallas_call(comm_kernel, out_shape=(shape((DIN, COL), F32), shape((DIN...]
where the time goes in v4:
time: 41.8 us; the launch traced here: 41.7 us
  Pallas kernels  41 us (98%)
  between operations  0.64 us (2%)
    pallas_call x1, Pallas kernels, local(): pl.pallas_call(comm_kernel, out_shape=(shape((DIN, COL), F32), shape((DIN...  39.7 us
    pallas_call x1, Pallas kernels, local(): pl.pallas_call(finish_kernel, out_shape=(shape((DIN, COL), F32), shape((D...  1.37 us

profile of v4, /device:TPU:8, one launch (start us, length us, event | category | flops | bytes accessed | tf_op | source)
XLA Modules:
  0.0 41.7 jit_solution(13778300756450602102)
XLA Ops:
  0.6 39.7 %powersgd_comm.1 = (f32[256,1024]{1,0:T(8,128)S(1)}, f32[256,1024]{1,0:T(8,128)S(1)}, f32[64,256]{1,0:T(8,128)S(1)}) custom-call(bf16[1024,256]{1,0:T(8,128)(2,1)} %acts_h.1, bf16[1024,1024]{1,0:T(8,128)(2,1)} %og_h.1, f32[256,1024]{1,0:T(8,128)} %w_h.1, f32[256,1024]{1,0:T(8,128)} %bitcast.3, f32[64,1024]{1,0:T(8,128)} %bitcast.4), custom_call_target="tpu_custom_call" | custom-call | tf_op jit(solution)/shard_map/powersgd_comm/pallas_call | solution.py:316
  40.3 1.4 %powersgd_finish.1 = (f32[256,1024]{1,0:T(8,128)}, f32[256,1024]{1,0:T(8,128)}, f32[64,256]{1,0:T(8,128)}) custom-call(f32[256,1024]{1,0:T(8,128)S(1)} %get-tuple-element.9.e_v, f32[256,1024]{1,0:T(8,128)S(1)} %get-tuple-element.10.w_v, f32[64,256]{1,0:T(8,128)S(1)} %get-tuple-element.11.ig_v), custom_call_target="tpu_custom_call" | custom-call | tf_op jit(solution)/shard_map/powersgd_finish/pallas_call | solution.py:359
